TPU v7x, 32 devices: a whole 2x2x4 slice. The times are simulated.
32 devices in a mesh: tm: 4 (over y, x), space: 8 (over z, core).
Axes of the slice: x: 2, y: 2, z: 4, core: 2. Of those that a mesh axis runs over, the one named last changes fastest.
Arguments:
- fields: bfloat16 [4096, 2, 16384], P('tm', None, 'space')
- calendar_day: int32 [4096], P('tm'), may hold values from 0 to 364, as said below
- events: int32 [16, 96], replicated, may hold values from 0 to 4080, as said below
- lag_offsets: int32 [16], replicated, may hold values from 0 to 15, each once
Outputs:
- composite: float32 [16, 16, 2, 16384], P('tm', None, None, 'space')
Inputs may be any that keep to these rules, and one draw needn't show every extreme that they name: `calendar_day`: days of the year of successive record days, one or two calendar days apart. `events`: each entry is a record day; a day may repeat within a type. `lag_offsets`: each of 0 to 15 once.
All inputs are finite; a program needn't handle non-finite values.
Results may differ from a plain program's by a relative error of at most 0.0012.
Values may be sent and summed in bfloat16 or wider, within the bound.
A program may use at most 64 MiB of HBM per device.

v0:
```python
import jax
import jax.numpy as jnp
from jax import lax
from jax.sharding import PartitionSpec as P

HARMONICS = 4
TWO_PI = 6.283185307179586


def regressors(calendar_day):
    phases = calendar_day.astype(jnp.float32) * (TWO_PI / 365.25)
    columns = [jnp.ones_like(phases)]
    for harmonic in range(1, HARMONICS + 1):
        columns.append(jnp.cos(harmonic * phases))
        columns.append(jnp.sin(harmonic * phases))
    return jnp.stack(columns, axis=1).astype(jnp.bfloat16)


def solve_fit(gram_matrix, projection):
    factor = jnp.linalg.cholesky(gram_matrix)
    return jax.scipy.linalg.cho_solve((factor, True), projection)


def fit_coefficients(gram_matrix, projection):
    gram_matrix, projection = lax.psum((gram_matrix, projection), "tm")
    return solve_fit(gram_matrix, projection)


def day_counts(events, lag_offsets, first_day, length):
    lag_count = lag_offsets.shape[0]
    day_numbers = first_day - (lag_count - 1) + lax.iota(jnp.int32, length + lag_count - 1)

    def type_histogram(event_row):
        matches = event_row[:, None] == day_numbers[None, :]
        return jnp.sum(matches.astype(jnp.float32), axis=0)

    histogram = lax.map(type_histogram, events).astype(jnp.bfloat16)
    shifted = jnp.stack(
        [
            lax.slice_in_dim(
                histogram, lag_count - 1 - offset, lag_count - 1 - offset + length, axis=1
            )
            for offset in range(lag_count)
        ]
    )
    lag_select = (lag_offsets[:, None] == lax.iota(jnp.int32, lag_count)[None, :]).astype(
        jnp.bfloat16
    )
    counts = jnp.einsum("ls,set->elt", lag_select, shifted, preferred_element_type=jnp.float32)
    return counts.astype(jnp.bfloat16).reshape(-1, length)


def shards(fields, calendar_day, events, lag_offsets):
    members = events.shape[1]
    lag_count = lag_offsets.shape[0]
    local_days = fields.shape[0]
    local_points = fields.shape[2]
    record = fields.reshape(local_days, 2 * local_points)
    design = regressors(calendar_day)
    gram_matrix = jnp.dot(design.T, design, preferred_element_type=jnp.float32)
    projection = jnp.dot(design.T, record, preferred_element_type=jnp.float32)
    counts = day_counts(events, lag_offsets, lax.axis_index("tm") * local_days, local_days)
    counted_design = jnp.dot(counts, design, preferred_element_type=jnp.float32)
    coefficients = fit_coefficients(gram_matrix, projection)
    raw_part = jnp.dot(counts, record, preferred_element_type=jnp.float32)
    totals = lax.psum_scatter(
        raw_part - jnp.dot(counted_design, coefficients, precision=lax.Precision.HIGHEST),
        "tm",
        scatter_dimension=0,
        tiled=True,
    )
    maps = (totals / members).reshape(-1, lag_count, 2, local_points)
    map_sums = lax.psum(jnp.sum(maps, axis=3, keepdims=True), "space")
    return maps - map_sums / (local_points * lax.axis_size("space"))


def solution(mesh):
    return jax.shard_map(
        shards,
        mesh=mesh,
        in_specs=(P("tm", None, "space"), P("tm"), P(), P()),
        out_specs=P("tm", None, None, "space"),
        check_vma=False,
    )
```

profile of v0, /device:TPU:0, one launch (start us, length us, event | category | flops | bytes accessed | tf_op | source)
XLA Modules:
  0.0 158.4 jit_solution(3301992195058840388)
XLA Ops:
  6.5 12.0 %copy.372 = bf16[128,8,2,2048]{3,1,2,0:T(8,128)(2,1)} copy(bf16[128,8,2,2048]{3,2,1,0:T(2,128)(2,1)} %bitcast.75) | data formatting | bytes 16777216
  18.6 0.1 sine_convert_fusion
  18.8 0.1 stack.112
  18.8 5.3 %fusion.14 = f32[9,4096]{1,0:T(8,128)} fusion(bf16[1024,9]{0,1:T(8,128)(2,1)S(1)} %stack.112, bf16[1024,4096]{1,0:T(8,128)(2,1)} %bitcast.73), kind=kOutput, calls=%fused_computation.55 | convolution fusion | flops 75497472 | bytes 8554496 | tf_op jit(solution)/shard_map/dot_general | solution.py:61
  24.2 0.1 fusion.13
  24.4 15.2 %while.11 = (s32[]{:T(128)}, bf16[16,1039]{1,0:T(8,128)(2,1)S(1)}, s32[16,96]{1,0:T(8,128)}, s32[]{:T(128)}, s32[]{:T(128)}, /*index=5*/s32[]{:T(128)}) while((s32[]{:T(128)}, bf16[16,1039]{1,0:T(8,128)(2,1)S(1)}, s32[16,96]{1,0:T(8,128)}, s32[]{:T(128)}, s32[]{:T(128)}, /*index=5*/s32[]{:T(128)}) %tuple.43), condition=%wide.region_2.3_spmd.clone, body=%wide.region_0.2_spmd.clone.sunk | while | flops 299234 | bytes 19943 | solution.py:37
  24.4 0.7 dynamic-slice_bitcast_fusion.2
  25.1 0.1 convert_reduce_fusion.2
  25.2 0.1 dynamic_update_slice.6
  25.3 0.7 dynamic-slice_bitcast_fusion.2
  26.0 0.1 convert_reduce_fusion.2
  26.2 0.1 dynamic_update_slice.6
  26.3 0.7 dynamic-slice_bitcast_fusion.2
  27.0 0.1 convert_reduce_fusion.2
  27.1 0.1 dynamic_update_slice.6
  27.2 0.7 dynamic-slice_bitcast_fusion.2
  27.9 0.1 convert_reduce_fusion.2
  28.2 0.7 dynamic-slice_bitcast_fusion.2
  28.9 0.1 convert_reduce_fusion.2
  29.1 0.7 dynamic-slice_bitcast_fusion.2
  29.8 0.1 convert_reduce_fusion.2
  30.1 0.7 dynamic-slice_bitcast_fusion.2
  30.8 0.1 convert_reduce_fusion.2
  31.0 0.7 dynamic-slice_bitcast_fusion.2
  31.7 0.1 convert_reduce_fusion.2
  32.0 0.7 dynamic-slice_bitcast_fusion.2
  32.7 0.1 convert_reduce_fusion.2
  32.9 0.7 dynamic-slice_bitcast_fusion.2
  33.6 0.1 convert_reduce_fusion.2
  33.9 0.7 dynamic-slice_bitcast_fusion.2
  34.6 0.1 convert_reduce_fusion.2
  34.8 0.7 dynamic-slice_bitcast_fusion.2
  35.5 0.1 convert_reduce_fusion.2
  35.8 0.7 dynamic-slice_bitcast_fusion.2
  36.5 0.1 convert_reduce_fusion.2
  36.7 0.7 dynamic-slice_bitcast_fusion.2
  37.4 0.1 convert_reduce_fusion.2
  37.7 0.7 dynamic-slice_bitcast_fusion.2
  38.4 0.1 convert_reduce_fusion.2
  38.6 0.7 dynamic-slice_bitcast_fusion.2
  39.3 0.1 convert_reduce_fusion.2
  39.5 0.2 slice_bitcast_fusion
  40.7 1.6 %stack.103 = bf16[16,16,1024]{2,0,1:T(8,128)(2,1)S(1)} concatenate(bf16[1,16,1024]{2,0,1:T(2,128)(2,1)S(1)} %copy.350, bf16[1,16,1024]{2,0,1:T(2,128)(2,1)S(1)} %copy.351, bf16[1,16,1024]{2,0,1:T(2,128)(2,1)S(1)} %copy.352, bf16[1,16,1024]{2,0,1:T(2,128)(2,1)S(1)} %copy.353, bf16[1,16,1024]{2,0,1:T(2,128)(2,1)S(1)} %copy.354, bf16[1,16,1024]{2,0,1:T(2,128)(2,1)S(1)} %copy.355, ...), dimensions={0} | concatenate | bytes 1048576 | tf_op jit(solution)/shard_map/stack | solution.py:38
  42.4 0.4 convolution_convert_fusion
  42.7 7.7 %fusion.11 = f32[256,4096]{1,0:T(8,128)} fusion(bf16[256,1024]{1,0:T(8,128)(2,1)S(1)} %bitcast.76, bf16[1024,4096]{1,0:T(8,128)(2,1)} %bitcast.74), kind=kOutput, calls=%fused_computation.52 | convolution fusion | flops 2147483648 | bytes 13107200 | tf_op jit(solution)/shard_map/dot_general | solution.py:65
  50.4 11.7 %psum.21 = f32[9,9]{0,1:T(8,128)S(1)} all-reduce(f32[9,9]{0,1:T(8,128)S(1)} %fusion.13), channel_id=1, replica_groups=mesh['tm'=4,'space'=8] {'tm'}, use_global_device_ids=true, to_apply=%region_3.4 | all-reduce | flops 81 | bytes 648 | tf_op jit(solution)/shard_map/psum | solution.py:25
  62.1 0.1 copy.367
  62.2 0.8 cholesky.16
  63.1 0.7 compare_reduce_fusion
  63.8 0.7 fusion.2
  64.5 0.7 custom-call.10
  65.2 0.2 fusion.12
  65.5 4.7 %all-reduce.2.cloned.1.call-done = f32[9,4096]{1,0:T(8,128)} async-done(((f32[9,4096]{1,0:T(8,128)}), f32[9,4096]{1,0:T(8,128)}) %all-reduce.2.cloned.1.call-update) | async-done | bytes 147472 | tf_op jit(solution)/shard_map/psum | solution.py:25
  70.1 1.4 fusion.3
  71.5 0.4 fusion.5
  71.8 6.6 %convolution_subtract_fusion = f32[256,4096]{1,0:T(8,128)} fusion(f32[256,4096]{1,0:T(8,128)} %fusion.11, f32[256,9]{0,1:T(8,128)S(1)} %fusion.12, f32[9,4096]{1,0:T(8,128)S(1)} %fusion.5), kind=kOutput, calls=%fused_computation.4 | convolution fusion | flops 114294784 | bytes 8545280 | tf_op jit(solution)/shard_map/dot_general | solution.py:67
  78.5 52.8 %reduce-scatter.2.cloned.1.call-done = f32[64,4096]{1,0:T(8,128)} async-done(((f32[256,4096]{1,0:T(8,128)}), f32[64,4096]{1,0:T(8,128)}) %reduce-scatter.2.cloned.1.call-update) | async-done | bytes 1048592 | tf_op jit(solution)/shard_map/reduce_scatter | solution.py:66
  131.3 1.3 broadcast_multiply_fusion
  132.6 0.9 reshape.28
  133.5 0.4 reduce_sum.18
  133.8 0.1 copy.369
  133.9 16.2 %psum.23 = f32[4,16,2,1]{1,0,3,2:T(4,128)S(1)} all-reduce(f32[4,16,2,1]{1,0,3,2:T(4,128)S(1)} %bitcast.78), channel_id=1, replica_groups=mesh['tm'=4,'space'=8] {'space'}, use_global_device_ids=true, to_apply=%region_9.10 | all-reduce | flops 128 | bytes 1024 | tf_op jit(solution)/shard_map/psum | solution.py:73
  150.1 0.1 copy.370
  150.2 1.4 broadcast_subtract_fusion
  (82 shorter events, 2.2 us)
Async XLA Ops:
  6.5 63.6 %all-reduce.2.cloned.1.call-start = ((), (), s32[]{:S(2)}) async-start(), calls=%async_computation.1 | async-start | bytes 524288 | tf_op jit(solution)/shard_map/psum | solution.py:25
  6.5 12.0 %copy-start = (s32[1024]{0:T(1024)S(1)}, s32[1024]{0:T(1024)}, u32[]{:S(2)}) copy-start(s32[1024]{0:T(1024)} %param.7) | copy-start | bytes 12292
  18.8 23.5 %copy-start.1 = (s32[16]{0:T(128)S(1)}, s32[16]{0:T(128)}, u32[]{:S(2)}) copy-start(s32[16]{0:T(128)} %param.9) | copy-start | bytes 196
  24.2 107.1 %reduce-scatter.2.cloned.1.call-start = ((), (), s32[]{:S(2)}) async-start(), calls=%async_computation.2 | async-start | bytes 5242880 | tf_op jit(solution)/shard_map/reduce_scatter | solution.py:66
Sparse Core Ops, SparseCore 0:
  24.3 45.7 all-reduce.1
  78.6 52.6 reduce-scatter.1
where the time goes:
time: 159 us; the launch traced here: 158 us
  waiting for transfers between devices  57.5 us (36%)
  local copies, waits for them, and re-layouts  28.5 us (18%)
  blocking collectives  27.9 us (18%)
  matrix products  22 us (14%)
  between operations  13.7 us (9%)
  other arithmetic  8.3 us (5%)
    reduce_scatter x1, waiting for transfers between devices, shards(): lax.psum_scatter(raw_part - jnp.dot(counted_design, coefficients, precisi...  52.8 us
    psum x1, blocking collectives, shards(): map_sums = lax.psum(jnp.sum(maps, axis=3, keepdims=True), 'space')  16.2 us
    unnamed x5, local copies, waits for them, and re-layouts  12 us
    psum x1, blocking collectives, fit_coefficients(): gram_matrix, projection = lax.psum((gram_matrix, projection), 'tm')  11.7 us
    eq x16, local copies, waits for them, and re-layouts, type_histogram(): matches = event_row[:, None] == day_numbers[None, :]  11.2 us
    dot_general x1, matrix products, shards(): raw_part = jnp.dot(counts, record, preferred_element_type=jnp.float32)  7.7 us
    dot_general x1, matrix products, shards(): jnp.dot(counted_design, coefficients, precision=lax.Precision.HIGHEST)  6.61 us
    dot_general x1, matrix products, shards(): projection = jnp.dot(design.T, record, preferred_element_type=jnp.float32)  5.3 us
  transfers between devices with their start and end apart: 2, of which 2 were waited for; matrix products, arithmetic and copies ran while one was open for 18% of the time, Pallas kernels for 0%

commit v1 on v0

--- a/solution.py
+++ b/solution.py
@@ -70,7 +70,7 @@
         tiled=True,
     )
     maps = (totals / members).reshape(-1, lag_count, 2, local_points)
-    map_sums = lax.psum(jnp.sum(maps, axis=3, keepdims=True), "space")
+    map_sums = jnp.sum(lax.all_gather(jnp.sum(maps, axis=3, keepdims=True), "space"), axis=0)
     return maps - map_sums / (local_points * lax.axis_size("space"))
 
 

time: 159 us -> 157 us (0.987)
  blocking collectives: 27.9 us -> 25.8 us
    psum x1 -> x0, blocking collectives: 16.2 us -> none  [shards(): map_sums = lax.psum(jnp.sum(maps, axis=3, keepdims=True), 'space')]
    all_gather x0 -> x1, blocking collectives: none -> 14.1 us  [shards(): lax.all_gather(jnp.sum(maps, axis=3, keepdims=True), 'space')]
where the time goes in v1:
time: 157 us; the launch traced here: 156 us
  waiting for transfers between devices  57.5 us (37%)
  local copies, waits for them, and re-layouts  28.5 us (18%)
  blocking collectives  25.8 us (16%)
  matrix products  22 us (14%)
  between operations  13.7 us (9%)
  other arithmetic  8.32 us (5%)
    reduce_scatter x1, waiting for transfers between devices, shards(): lax.psum_scatter(raw_part - jnp.dot(counted_design, coefficients, precisi...  52.8 us
    all_gather x1, blocking collectives, shards(): lax.all_gather(jnp.sum(maps, axis=3, keepdims=True), 'space')  14.1 us
    unnamed x5, local copies, waits for them, and re-layouts  12 us
    psum x1, blocking collectives, fit_coefficients(): gram_matrix, projection = lax.psum((gram_matrix, projection), 'tm')  11.7 us
    eq x16, local copies, waits for them, and re-layouts, type_histogram(): matches = event_row[:, None] == day_numbers[None, :]  11.2 us
    dot_general x1, matrix products, shards(): raw_part = jnp.dot(counts, record, preferred_element_type=jnp.float32)  7.7 us
    dot_general x1, matrix products, shards(): jnp.dot(counted_design, coefficients, precision=lax.Precision.HIGHEST)  6.61 us
    dot_general x1, matrix products, shards(): projection = jnp.dot(design.T, record, preferred_element_type=jnp.float32)  5.3 us
  transfers between devices with their start and end apart: 2, of which 2 were waited for; matrix products, arithmetic and copies ran while one was open for 18% of the time, Pallas kernels for 0%

profile of v1, /device:TPU:0, one launch (start us, length us, event | category | flops | bytes accessed | tf_op | source)
XLA Modules:
  0.0 156.4 jit_solution(2694736856170568575)
XLA Ops:
  6.5 12.0 %copy.396 = bf16[128,8,2,2048]{3,1,2,0:T(8,128)(2,1)} copy(bf16[128,8,2,2048]{3,2,1,0:T(2,128)(2,1)} %bitcast.73) | data formatting | bytes 16777216
  18.6 0.1 sine_convert_fusion
  18.8 0.1 stack.112
  18.8 5.3 %fusion.14 = f32[9,4096]{1,0:T(8,128)} fusion(bf16[1024,9]{0,1:T(8,128)(2,1)S(1)} %stack.112, bf16[1024,4096]{1,0:T(8,128)(2,1)} %bitcast.71), kind=kOutput, calls=%fused_computation.55 | convolution fusion | flops 75497472 | bytes 8554496 | tf_op jit(solution)/shard_map/dot_general | solution.py:61
  24.2 0.1 fusion.13
  24.4 15.2 %while.11 = (s32[]{:T(128)}, bf16[16,1039]{1,0:T(8,128)(2,1)S(1)}, s32[16,96]{1,0:T(8,128)}, s32[]{:T(128)}, s32[]{:T(128)}, /*index=5*/s32[]{:T(128)}) while((s32[]{:T(128)}, bf16[16,1039]{1,0:T(8,128)(2,1)S(1)}, s32[16,96]{1,0:T(8,128)}, s32[]{:T(128)}, s32[]{:T(128)}, /*index=5*/s32[]{:T(128)}) %tuple.43), condition=%wide.region_2.3_spmd.clone, body=%wide.region_0.2_spmd.clone.sunk | while | flops 299234 | bytes 19943 | solution.py:37
  24.4 0.7 dynamic-slice_bitcast_fusion.2
  25.1 0.1 convert_reduce_fusion.2
  25.2 0.1 dynamic_update_slice.6
  25.3 0.7 dynamic-slice_bitcast_fusion.2
  26.0 0.1 convert_reduce_fusion.2
  26.2 0.1 dynamic_update_slice.6
  26.3 0.7 dynamic-slice_bitcast_fusion.2
  27.0 0.1 convert_reduce_fusion.2
  27.1 0.1 dynamic_update_slice.6
  27.2 0.7 dynamic-slice_bitcast_fusion.2
  27.9 0.1 convert_reduce_fusion.2
  28.2 0.7 dynamic-slice_bitcast_fusion.2
  28.9 0.1 convert_reduce_fusion.2
  29.1 0.7 dynamic-slice_bitcast_fusion.2
  29.8 0.1 convert_reduce_fusion.2
  30.1 0.7 dynamic-slice_bitcast_fusion.2
  30.8 0.1 convert_reduce_fusion.2
  31.0 0.7 dynamic-slice_bitcast_fusion.2
  31.7 0.1 convert_reduce_fusion.2
  32.0 0.7 dynamic-slice_bitcast_fusion.2
  32.7 0.1 convert_reduce_fusion.2
  32.9 0.7 dynamic-slice_bitcast_fusion.2
  33.6 0.1 convert_reduce_fusion.2
  33.9 0.7 dynamic-slice_bitcast_fusion.2
  34.6 0.1 convert_reduce_fusion.2
  34.8 0.7 dynamic-slice_bitcast_fusion.2
  35.5 0.1 convert_reduce_fusion.2
  35.8 0.7 dynamic-slice_bitcast_fusion.2
  36.5 0.1 convert_reduce_fusion.2
  36.7 0.7 dynamic-slice_bitcast_fusion.2
  37.4 0.1 convert_reduce_fusion.2
  37.7 0.7 dynamic-slice_bitcast_fusion.2
  38.4 0.1 convert_reduce_fusion.2
  38.6 0.7 dynamic-slice_bitcast_fusion.2
  39.3 0.1 convert_reduce_fusion.2
  39.5 0.2 slice_bitcast_fusion
  40.7 1.6 %stack.103 = bf16[16,16,1024]{2,0,1:T(8,128)(2,1)S(1)} concatenate(bf16[1,16,1024]{2,0,1:T(2,128)(2,1)S(1)} %copy.373, bf16[1,16,1024]{2,0,1:T(2,128)(2,1)S(1)} %copy.374, bf16[1,16,1024]{2,0,1:T(2,128)(2,1)S(1)} %copy.375, bf16[1,16,1024]{2,0,1:T(2,128)(2,1)S(1)} %copy.376, bf16[1,16,1024]{2,0,1:T(2,128)(2,1)S(1)} %copy.377, bf16[1,16,1024]{2,0,1:T(2,128)(2,1)S(1)} %copy.378, ...), dimensions={0} | concatenate | bytes 1048576 | tf_op jit(solution)/shard_map/stack | solution.py:38
  42.4 0.4 convolution_convert_fusion
  42.7 7.7 %fusion.11 = f32[256,4096]{1,0:T(8,128)} fusion(bf16[256,1024]{1,0:T(8,128)(2,1)S(1)} %bitcast.74, bf16[1024,4096]{1,0:T(8,128)(2,1)} %bitcast.72), kind=kOutput, calls=%fused_computation.52 | convolution fusion | flops 2147483648 | bytes 13107200 | tf_op jit(solution)/shard_map/dot_general | solution.py:65
  50.4 11.7 %psum.14 = f32[9,9]{0,1:T(8,128)S(1)} all-reduce(f32[9,9]{0,1:T(8,128)S(1)} %fusion.13), channel_id=1, replica_groups=mesh['tm'=4,'space'=8] {'tm'}, use_global_device_ids=true, to_apply=%region_3.4 | all-reduce | flops 81 | bytes 648 | tf_op jit(solution)/shard_map/psum | solution.py:25
  62.1 0.1 copy.390
  62.2 0.8 cholesky.16
  63.1 0.7 compare_reduce_fusion
  63.8 0.7 fusion.2
  64.5 0.7 custom-call.10
  65.2 0.2 fusion.12
  65.5 4.7 %all-reduce.2.cloned.1.call-done = f32[9,4096]{1,0:T(8,128)} async-done(((f32[9,4096]{1,0:T(8,128)}), f32[9,4096]{1,0:T(8,128)}) %all-reduce.2.cloned.1.call-update) | async-done | bytes 147472 | tf_op jit(solution)/shard_map/psum | solution.py:25
  70.1 1.4 fusion.3
  71.5 0.4 fusion.5
  71.8 6.6 %convolution_subtract_fusion = f32[256,4096]{1,0:T(8,128)} fusion(f32[256,4096]{1,0:T(8,128)} %fusion.11, f32[256,9]{0,1:T(8,128)S(1)} %fusion.12, f32[9,4096]{1,0:T(8,128)S(1)} %fusion.5), kind=kOutput, calls=%fused_computation.4 | convolution fusion | flops 114294784 | bytes 8545280 | tf_op jit(solution)/shard_map/dot_general | solution.py:67
  78.5 52.8 %reduce-scatter.2.cloned.1.call-done = f32[64,4096]{1,0:T(8,128)} async-done(((f32[256,4096]{1,0:T(8,128)}), f32[64,4096]{1,0:T(8,128)}) %reduce-scatter.2.cloned.1.call-update) | async-done | bytes 1048592 | tf_op jit(solution)/shard_map/reduce_scatter | solution.py:66
  131.3 1.3 broadcast_multiply_fusion
  132.6 0.9 reshape.33
  133.5 0.4 reduce_sum.27
  133.8 0.1 copy.392
  133.9 14.1 %all-gather = f32[32,16,2]{1,2,0:T(2,128)S(1)} all-gather(f32[4,16,2]{1,2,0:T(2,128)S(1)} %copy.392), channel_id=2, replica_groups=mesh['tm'=4,'space'=8] {'space'}, dimensions={0}, use_global_device_ids=true | all-gather | bytes 4608 | tf_op jit(solution)/shard_map/all_gather | solution.py:73
  148.1 0.1 copy.394
  148.2 1.4 broadcast_subtract_fusion
  (83 shorter events, 2.2 us)
Async XLA Ops:
  6.5 63.6 %all-reduce.2.cloned.1.call-start = ((), (), s32[]{:S(2)}) async-start(), calls=%async_computation.1 | async-start | bytes 524288 | tf_op jit(solution)/shard_map/psum | solution.py:25
  6.5 12.0 %copy-start = (s32[1024]{0:T(1024)S(1)}, s32[1024]{0:T(1024)}, u32[]{:S(2)}) copy-start(s32[1024]{0:T(1024)} %param.7) | copy-start | bytes 12292
  18.8 23.5 %copy-start.1 = (s32[16]{0:T(128)S(1)}, s32[16]{0:T(128)}, u32[]{:S(2)}) copy-start(s32[16]{0:T(128)} %param.9) | copy-start | bytes 196
  24.2 107.1 %reduce-scatter.2.cloned.1.call-start = ((), (), s32[]{:S(2)}) async-start(), calls=%async_computation.2 | async-start | bytes 5242880 | tf_op jit(solution)/shard_map/reduce_scatter | solution.py:66
Sparse Core Ops, SparseCore 0:
  24.3 45.7 all-reduce.1
  78.6 52.6 reduce-scatter.1
